TPU v7x, 32 devices: a whole 2x2x4 slice. The times are simulated.
32 devices in a mesh: expert: 8 (over z, x), shard: 4 (over y, core).
Axes of the slice: x: 2, y: 2, z: 4, core: 2. Of those that a mesh axis runs over, the one named last changes fastest.
Arguments:
- train_down: float32 [16, 6400, 4096], P('expert', None, 'shard'), may hold values from -0.109375 to 0.109375
- router_weight: float32 [4096, 16], P('shard', 'expert'), may hold values from -0.09375 to 0.09375
- router_gain: float32 [4096], P('shard'), may hold values from 0.25 to 1.75
Outputs:
- ready_down: bfloat16 [16, 6400, 4096], P('expert', 'shard')
- scale_down: float32 [16, 6400], P('expert', 'shard')
- serve_router: bfloat16 [4096, 16], replicated
All inputs are finite; a program needn't handle non-finite values. Where the computation divides by a largest or mean magnitude, that divisor is 1e-20 or more.
Results may differ from a plain program's by a relative error of at most 0.001.
Values may be sent and summed in bfloat16 or wider, within the bound.
A program may use at most 192 MiB of HBM per device.

v0:
```python
import jax
import jax.numpy as jnp
from jax import lax
from jax.sharding import PartitionSpec as P


def per_device(train_down, router_weight, router_gain):
    scale_down = lax.pmax(jnp.max(jnp.abs(train_down), axis=2), "shard")
    narrow_down = (train_down / jnp.expand_dims(scale_down, 2)).astype(jnp.bfloat16)
    ready_down = lax.all_to_all(narrow_down, "shard", split_axis=1, concat_axis=2, tiled=True)
    scale_down = lax.dynamic_slice_in_dim(
        scale_down, lax.axis_index("shard") * ready_down.shape[1], ready_down.shape[1], axis=1
    )
    part_router = (router_weight * router_gain[:, None]).astype(jnp.bfloat16)
    row_router = lax.all_gather(part_router, "shard", axis=0, tiled=True)
    serve_router = lax.all_gather(row_router, "expert", axis=1, tiled=True)
    return (ready_down, scale_down, serve_router)


def solution(mesh):
    in_specs = (P("expert", None, "shard"), P("shard", "expert"), P("shard"))
    out_specs = (P("expert", "shard", None), P("expert", "shard"), P())
    return jax.shard_map(
        per_device, mesh=mesh, in_specs=in_specs, out_specs=out_specs, check_vma=False
    )
```

profile of v0, /device:TPU:0, one launch (start us, length us, event | category | flops | bytes accessed | tf_op | source)
XLA Modules:
  0.0 506.3 jit_solution(6970151837764628725)
XLA Ops:
  0.6 17.0 %abs_reduce_fusion = f32[2,6400]{1,0:T(2,128)S(1)} fusion(f32[2,6400,1024]{2,1,0:T(8,128)} %param.3), kind=kLoop, calls=%fused_computation.1 | loop fusion | flops 26201600 | bytes 52480000 | tf_op jit(solution)/shard_map/reduce_max | solution.py:8
  17.6 13.4 %pmax.7 = f32[2,6400]{1,0:T(2,128)S(1)} all-reduce(f32[2,6400]{1,0:T(2,128)S(1)} %abs_reduce_fusion), channel_id=1, replica_groups=mesh['expert'=8,'shard'=4] {'shard'}, use_global_device_ids=true, to_apply=%region_1.0 | all-reduce | flops 12800 | bytes 102400 | tf_op jit(solution)/shard_map/pmax | solution.py:8
  31.1 26.1 %divide_convert_fusion = bf16[2,6400,1024]{2,1,0:T(8,128)(2,1)} fusion(f32[2,6400,1024]{2,1,0:T(8,128)} %param.3, f32[2,6400]{1,0:T(2,128)S(1)} %pmax.7), kind=kLoop, calls=%fused_computation | loop fusion | flops 26214400 | bytes 78694400 | tf_op jit(solution)/shard_map/convert_element_type | solution.py:9
  57.2 0.0 copy-start
  57.2 0.0 copy-start.1
  57.2 47.4 %copy.10 = bf16[2,6400,1024]{2,0,1:T(2,128)(2,1)} copy(bf16[2,6400,1024]{2,1,0:T(8,128)(2,1)} %divide_convert_fusion) | data formatting | bytes 52428800 | tf_op jit(solution)/shard_map/convert_element_type | solution.py:9
  104.6 8.6 %all-to-all-start = ((bf16[2,6400,1024]{2,0,1:T(2,128)(2,1)}), bf16[2,6400,1024]{2,0,1:T(2,128)(2,1)}, u32[]{:S(2)}, u32[]{:S(2)}) async-start(bf16[2,6400,1024]{2,0,1:T(2,128)(2,1)} %copy.10), calls=%async_computation | async-start | bytes 52428800 | tf_op jit(solution)/shard_map/all_to_all | solution.py:10
  113.2 0.0 copy-done
  113.2 0.0 copy-done.1
  113.2 285.0 %all_gather.6 = bf16[4096,2]{0,1:T(2,128)(2,1)S(1)} all-gather(bf16[1024,2]{0,1:T(2,128)(2,1)S(1)} %multiply_convert_fusion), channel_id=1, replica_groups=mesh['expert'=8,'shard'=4] {'shard'}, dimensions={0}, use_global_device_ids=true | all-gather | bytes 20480 | tf_op jit(solution)/shard_map/all_gather | solution.py:15
  398.2 30.8 %all-gather = bf16[8,2,4096]{2,1,0:T(2,128)(2,1)S(1)} all-gather(bf16[1,2,4096]{2,1,0:T(2,128)(2,1)S(1)} %bitcast.8), channel_id=1, replica_groups=mesh['expert'=8,'shard'=4] {'expert'}, dimensions={0}, use_global_device_ids=true | all-gather | bytes 147456 | tf_op jit(solution)/shard_map/all_gather | solution.py:16
  429.1 0.7 reshape.9
  429.8 0.7 constant_dynamic-slice_fusion
  430.5 0.0 all-to-all-done
  430.5 33.4 %copy.11 = bf16[2,1600,4,1024]{3,2,1,0:T(4,128)(2,1)} copy(bf16[2,1600,4,1024]{3,0,1,2:T(2,128)(2,1)} %bitcast.1) | data formatting | bytes 52428800 | tf_op jit(solution)/shard_map/all_to_all | solution.py:10
  463.8 42.5 %all_to_all.16 = bf16[2,1600,4096]{2,1,0:T(8,128)(2,1)} reshape(bf16[2,1600,4,1024]{3,2,1,0:T(4,128)(2,1)} %copy.11) | data formatting | bytes 52428800 | tf_op jit(solution)/shard_map/all_to_all | solution.py:10
  (1 shorter events, 0.0 us)
Async XLA Ops:
  57.2 56.0 %copy-start = (f32[1024,2]{0,1:T(2,128)S(1)}, f32[1024,2]{0,1:T(2,128)}, u32[]{:S(2)}) copy-start(f32[1024,2]{0,1:T(2,128)} %param.4) | copy-start | bytes 24580
  57.2 56.0 %copy-start.1 = (f32[1024]{0:T(1024)S(1)}, f32[1024]{0:T(1024)}, u32[]{:S(2)}) copy-start(f32[1024]{0:T(1024)} %param.5) | copy-start | bytes 12292
  104.6 325.9 %all-to-all-start = ((bf16[2,6400,1024]{2,0,1:T(2,128)(2,1)}), bf16[2,6400,1024]{2,0,1:T(2,128)(2,1)}, u32[]{:S(2)}, u32[]{:S(2)}) async-start(bf16[2,6400,1024]{2,0,1:T(2,128)(2,1)} %copy.10), calls=%async_computation | async-start | bytes 52428800 | tf_op jit(solution)/shard_map/all_to_all | solution.py:10
where the time goes:
time: 508 us; the launch traced here: 506 us
  blocking collectives  329 us (65%)
  local copies, waits for them, and re-layouts  125 us (25%)
  other arithmetic  43.2 us (9%)
  starting transfers between devices  8.59 us (2%)
    all_gather x1, blocking collectives, per_device(): row_router = lax.all_gather(part_router, 'shard', axis=0, tiled=True)  285 us
    all_to_all x2, local copies, waits for them, and re-layouts, per_device(): lax.all_to_all(narrow_down, 'shard', split_axis=1, concat_axis=2, tiled=T...  75.8 us
    convert_element_type x1, local copies, waits for them, and re-layouts, per_device(): (train_down / jnp.expand_dims(scale_down, 2)).astype(jnp.bfloat16)  47.4 us
    all_gather x1, blocking collectives, per_device(): serve_router = lax.all_gather(row_router, 'expert', axis=1, tiled=True)  30.8 us
    convert_element_type x1, other arithmetic, per_device(): (train_down / jnp.expand_dims(scale_down, 2)).astype(jnp.bfloat16)  26.1 us
    reduce_max x1, other arithmetic, per_device(): scale_down = lax.pmax(jnp.max(jnp.abs(train_down), axis=2), 'shard')  17 us
    pmax x1, blocking collectives, per_device(): scale_down = lax.pmax(jnp.max(jnp.abs(train_down), axis=2), 'shard')  13.4 us
  transfers between devices with their start and end apart: 1, of which 0 were waited for; matrix products, arithmetic and copies ran while one was open for 0% of the time, Pallas kernels for 0%

commit v1 on v0

--- a/solution.py
+++ b/solution.py
@@ -4,10 +4,26 @@
 from jax.sharding import PartitionSpec as P
 
 
+def swapped_with_each(value, axis, split, join):
+    ways, here = (lax.axis_size(axis), lax.axis_index(axis))
+    width = value.shape[split] // ways
+    shape = list(value.shape)
+    shape[split] = width
+    height = shape[join]
+    shape[join] = height * ways
+    full = jnp.zeros(shape, value.dtype)
+    for mask in range(ways):
+        part = lax.dynamic_slice_in_dim(value, (here ^ mask) * width, width, axis=split)
+        if mask:
+            part = lax.ppermute(part, axis, [(d, d ^ mask) for d in range(ways)])
+        full = lax.dynamic_update_slice_in_dim(full, part, (here ^ mask) * height, axis=join)
+    return full
+
+
 def per_device(train_down, router_weight, router_gain):
     scale_down = lax.pmax(jnp.max(jnp.abs(train_down), axis=2), "shard")
     narrow_down = (train_down / jnp.expand_dims(scale_down, 2)).astype(jnp.bfloat16)
-    ready_down = lax.all_to_all(narrow_down, "shard", split_axis=1, concat_axis=2, tiled=True)
+    ready_down = swapped_with_each(narrow_down, "shard", 1, 2)
     scale_down = lax.dynamic_slice_in_dim(
         scale_down, lax.axis_index("shard") * ready_down.shape[1], ready_down.shape[1], axis=1
     )

time: 508 us -> 422 us (0.83)
  local copies, waits for them, and re-layouts: 125 us -> 48.7 us
  starting transfers between devices: 8.59 us -> 1.86 us
    all_to_all x2 -> x0, local copies, waits for them, and re-layouts: 75.8 us -> none  [per_device(): lax.all_to_all(narrow_down, 'shard', split_axis=1, concat_axis=2, tiled=T...]
    convert_element_type x1 -> x0, local copies, waits for them, and re-layouts: 47.4 us -> none  [per_device(): (train_down / jnp.expand_dims(scale_down, 2)).astype(jnp.bfloat16)]
    dynamic_update_slice x0 -> x3, local copies, waits for them, and re-layouts: none -> 19.2 us  [swapped_with_each(): lax.dynamic_update_slice_in_dim(full, part, (here ^ mask) * height, axis=...]
    dynamic_slice x0 -> x1, local copies, waits for them, and re-layouts: none -> 19.2 us  [swapped_with_each(): lax.dynamic_slice_in_dim(value, (here ^ mask) * width, width, axis=split)]
    broadcast_in_dim x0 -> x1, local copies, waits for them, and re-layouts: none -> 8.97 us  [swapped_with_each(): full = jnp.zeros(shape, value.dtype)]
    all_to_all x1 -> x0, starting transfers between devices: 8.59 us -> none  [per_device(): lax.all_to_all(narrow_down, 'shard', split_axis=1, concat_axis=2, tiled=T...]
  transfers between devices with their start and end apart: 1 -> 3, of which waited for: 0 -> 0; matrix products, arithmetic and copies ran while one was open for 0% -> 3% of each run, Pallas kernels for 0% -> 0%
where the time goes in v1:
time: 422 us
  blocking collectives  328 us (78%)
  local copies, waits for them, and re-layouts  48.7 us (12%)
  other arithmetic  43.2 us (10%)
    all_gather x1, blocking collectives, per_device(): row_router = lax.all_gather(part_router, 'shard', axis=0, tiled=True)  283 us
    all_gather x1, blocking collectives, per_device(): serve_router = lax.all_gather(row_router, 'expert', axis=1, tiled=True)  30.8 us
    convert_element_type x1, other arithmetic, per_device(): (train_down / jnp.expand_dims(scale_down, 2)).astype(jnp.bfloat16)  26.2 us
    dynamic_update_slice x3, local copies, waits for them, and re-layouts, swapped_with_each(): lax.dynamic_update_slice_in_dim(full, part, (here ^ mask) * height, axis=...  19.2 us
    dynamic_slice x1, local copies, waits for them, and re-layouts, swapped_with_each(): lax.dynamic_slice_in_dim(value, (here ^ mask) * width, width, axis=split)  19.2 us
    reduce_max x1, other arithmetic, per_device(): scale_down = lax.pmax(jnp.max(jnp.abs(train_down), axis=2), 'shard')  17 us
    pmax x1, blocking collectives, per_device(): scale_down = lax.pmax(jnp.max(jnp.abs(train_down), axis=2), 'shard')  13.4 us
    broadcast_in_dim x1, local copies, waits for them, and re-layouts, swapped_with_each(): full = jnp.zeros(shape, value.dtype)  8.97 us
  transfers between devices with their start and end apart: 3, of which 0 were waited for; matrix products, arithmetic and copies ran while one was open for 3% of the time, Pallas kernels for 0%

profile of v1, /device:TPU:0, one launch (start us, length us, event | category | flops | bytes accessed | tf_op | source)
XLA Modules:
  0.0 422.1 jit_solution(469577618475261511)
XLA Ops:
  0.6 17.0 %abs_reduce_fusion = f32[2,6400]{1,0:T(2,128)S(1)} fusion(f32[2,6400,1024]{2,1,0:T(8,128)} %param.3), kind=kLoop, calls=%fused_computation.1 | loop fusion | flops 26201600 | bytes 52480000 | tf_op jit(solution)/shard_map/reduce_max | solution.py:24
  17.7 13.4 %pmax.7 = f32[2,6400]{1,0:T(2,128)S(1)} all-reduce(f32[2,6400]{1,0:T(2,128)S(1)} %abs_reduce_fusion), channel_id=1, replica_groups=mesh['expert'=8,'shard'=4] {'shard'}, use_global_device_ids=true, to_apply=%region_1.0 | all-reduce | flops 12800 | bytes 102400 | tf_op jit(solution)/shard_map/pmax | solution.py:24
  31.1 26.2 %divide_convert_fusion = bf16[2,6400,1024]{2,1,0:T(8,128)(2,1)} fusion(f32[2,6400,1024]{2,1,0:T(8,128)} %param.3, f32[2,6400]{1,0:T(2,128)S(1)} %pmax.7), kind=kLoop, calls=%fused_computation | loop fusion | flops 26214400 | bytes 78694400 | tf_op jit(solution)/shard_map/convert_element_type | solution.py:25
  57.3 9.0 %broadcast_in_dim.2 = bf16[2,1600,4096]{2,1,0:T(8,128)(2,1)} broadcast(bf16[]{:T(256)} %constant.11.clone.1), dimensions={} | broadcast | bytes 26214402 | tf_op jit(solution)/shard_map/broadcast_in_dim | solution.py:14
  66.3 0.0 copy-start
  66.3 0.0 copy-start.1
  66.3 19.2 %constant_dynamic-slice_fusion = (bf16[2,1600,1024]{2,1,0:T(8,128)(2,1)}, bf16[2,1600,1024]{2,1,0:T(8,128)(2,1)}, bf16[2,1600,1024]{2,1,0:T(8,128)(2,1)}, bf16[2,1600,4096]{2,1,0:T(8,128)(2,1)}) fusion(bf16[2,6400,1024]{2,1,0:T(8,128)(2,1)} %divide_convert_fusion, s32[]{:T(128)S(6)} %select_n.31, s32[]{:T(128)S(6)} %select_n.29, s32[]{:T(128)S(6)} %select_n.27, ...), kind=kLoop, calls=%fused_computation.5 | loop fusion | bytes 52428820 | tf_op jit(solution)/shard_map/dynamic_slice | solution.py:16
  85.4 0.0 collective-permute-start
  85.4 0.4 collective-permute-start.1
  85.9 1.4 collective-permute-start.2
  87.3 0.0 copy-done
  87.3 0.0 copy-done.1
  87.3 283.3 %all_gather.6 = bf16[4096,2]{0,1:T(2,128)(2,1)S(1)} all-gather(bf16[1024,2]{0,1:T(2,128)(2,1)S(1)} %multiply_convert_fusion), channel_id=1, replica_groups=mesh['expert'=8,'shard'=4] {'shard'}, dimensions={0}, use_global_device_ids=true | all-gather | bytes 20480 | tf_op jit(solution)/shard_map/all_gather | solution.py:31
  370.6 30.8 %all-gather = bf16[8,2,4096]{2,1,0:T(2,128)(2,1)S(1)} all-gather(bf16[1,2,4096]{2,1,0:T(2,128)(2,1)S(1)} %bitcast.5), channel_id=1, replica_groups=mesh['expert'=8,'shard'=4] {'expert'}, dimensions={0}, use_global_device_ids=true | all-gather | bytes 147456 | tf_op jit(solution)/shard_map/all_gather | solution.py:32
  401.5 0.7 reshape.9
  402.2 0.7 constant_dynamic-slice_fusion.3
  402.9 0.0 collective-permute-done
  402.9 6.4 %constant_dynamic-update-slice_fusion.2 = bf16[2,1600,4096]{2,1,0:T(8,128)(2,1)} fusion(bf16[2,1600,4096]{2,1,0:T(8,128)(2,1)} %get-tuple-element.6, bf16[2,1600,1024]{2,1,0:T(8,128)(2,1)} %collective-permute-done, s32[]{:T(128)S(6)} %select_n.28), kind=kLoop, calls=%fused_computation.8 | loop fusion | bytes 13107204 | tf_op jit(solution)/shard_map/dynamic_update_slice | solution.py:19
  409.3 0.0 collective-permute-done.1
  409.3 6.4 %constant_dynamic-update-slice_fusion.1 = bf16[2,1600,4096]{2,1,0:T(8,128)(2,1)} fusion(bf16[2,1600,4096]{2,1,0:T(8,128)(2,1)} %constant_dynamic-update-slice_fusion.2, bf16[2,1600,1024]{2,1,0:T(8,128)(2,1)} %collective-permute-done.1, s32[]{:T(128)S(6)} %select_n.30), kind=kLoop, calls=%fused_computation.6 | loop fusion | bytes 13107204 | tf_op jit(solution)/shard_map/dynamic_update_slice | solution.py:19
  415.7 0.0 collective-permute-done.2
  415.7 6.4 %constant_dynamic-update-slice_fusion = bf16[2,1600,4096]{2,1,0:T(8,128)(2,1)} fusion(bf16[2,1600,4096]{2,1,0:T(8,128)(2,1)} %constant_dynamic-update-slice_fusion.1, bf16[2,1600,1024]{2,1,0:T(8,128)(2,1)} %collective-permute-done.2, s32[]{:T(128)S(6)} %select_n.32), kind=kLoop, calls=%fused_computation.4 | loop fusion | bytes 13107204 | tf_op jit(solution)/shard_map/dynamic_update_slice | solution.py:19
  (1 shorter events, 0.0 us)
Async XLA Ops:
  66.3 21.0 %copy-start = (f32[1024,2]{0,1:T(2,128)S(1)}, f32[1024,2]{0,1:T(2,128)}, u32[]{:S(2)}) copy-start(f32[1024,2]{0,1:T(2,128)} %param.4) | copy-start | bytes 24580
  66.3 21.0 %copy-start.1 = (f32[1024]{0:T(1024)S(1)}, f32[1024]{0:T(1024)}, u32[]{:S(2)}) copy-start(f32[1024]{0:T(1024)} %param.5) | copy-start | bytes 12292
  85.4 317.5 %collective-permute-start = (bf16[2,1600,1024]{2,1,0:T(8,128)(2,1)}, bf16[2,1600,1024]{2,1,0:T(8,128)(2,1)}, u32[]{:S(2)}, u32[]{:S(2)}) collective-permute-start(bf16[2,1600,1024]{2,1,0:T(8,128)(2,1)} %get-tuple-element.5), channel_id=1, source_target_pairs={{0,1},{1,0},{2,3},{3,2},{4,5},{5,4},{6,7},{7,6},{8,9},{9,8},{10,11... | collective-permute-start | bytes 19660808 | tf_op jit(solution)/shard_map/ppermute | solution.py:18
  85.4 323.8 %collective-permute-start.1 = (bf16[2,1600,1024]{2,1,0:T(8,128)(2,1)}, bf16[2,1600,1024]{2,1,0:T(8,128)(2,1)}, u32[]{:S(2)}, u32[]{:S(2)}) collective-permute-start(bf16[2,1600,1024]{2,1,0:T(8,128)(2,1)} %get-tuple-element.4), channel_id=1, source_target_pairs={{0,2},{1,3},{2,0},{3,1},{4,6},{5,7},{6,4},{7,5},{8,10},{9,11},{10,... | collective-permute-start | bytes 19660808 | tf_op jit(solution)/shard_map/ppermute | solution.py:18
  85.9 329.8 %collective-permute-start.2 = (bf16[2,1600,1024]{2,1,0:T(8,128)(2,1)}, bf16[2,1600,1024]{2,1,0:T(8,128)(2,1)}, u32[]{:S(2)}, u32[]{:S(2)}) collective-permute-start(bf16[2,1600,1024]{2,1,0:T(8,128)(2,1)} %get-tuple-element.3), channel_id=1, source_target_pairs={{0,3},{1,2},{2,1},{3,0},{4,7},{5,6},{6,5},{7,4},{8,11},{9,10},{10,... | collective-permute-start | bytes 19660808 | tf_op jit(solution)/shard_map/ppermute | solution.py:18
